TPU v7x, 32 devices: a whole 2x2x4 slice. The times are simulated.
32 devices in a mesh: rep: 2 (over x), exp: 16 (over z, y, core).
Axes of the slice: x: 2, y: 2, z: 4, core: 2. Of those that a mesh axis runs over, the one named last changes fastest.
Arguments:
- a_tokens: bfloat16 [64, 7168], P(('rep', 'exp')), parts along dimension 0, may hold values from -6 to 6
- a_gain: float32 [7168], replicated, may hold values from 0.25 to 1.75
- dense_gate: bfloat16 [7168, 18432], P(None, 'exp'), may hold values from -0.0625 to 0.0625
- dense_up: bfloat16 [7168, 18432], P(None, 'exp'), may hold values from -0.0625 to 0.0625
- dense_down: bfloat16 [18432, 7168], P('exp'), may hold values from -0.046875 to 0.046875
- b_tokens: bfloat16 [128, 7168], P(('rep', 'exp')), parts along dimension 0, may hold values from -6 to 6
- b_gain: float32 [7168], replicated, may hold values from 0.25 to 1.75
- expert_ids: int32 [128, 8], P(('rep', 'exp')), parts along dimension 0, may hold values from 0 to 15, all different within a row; in each aligned block of 4 rows (0 to 3, 4 to 7, ...) at most 3 rows name the same one
- route_weights: float32 [128, 8], P(('rep', 'exp')), parts along dimension 0, may hold values from 0.05 to 0.5
- expert_gate: bfloat16 [16, 7168, 1024], P('exp'), may hold values from -0.0625 to 0.0625
- expert_up: bfloat16 [16, 7168, 1024], P('exp'), may hold values from -0.0625 to 0.0625
- expert_down: bfloat16 [16, 1024, 7168], P('exp'), may hold values from -0.1875 to 0.1875
Outputs:
- a_out: bfloat16 [64, 7168], P(('rep', 'exp')), parts along dimension 0
- b_out: bfloat16 [128, 7168], P(('rep', 'exp')), parts along dimension 0
There are 2 independent parts, one for each index of `rep`. A program takes and returns all parts, laid end to end along the dimension named above; an argument that names none is the same for every part. Nothing has to cross between parts.
Inputs may be any that keep to these rules, and one draw needn't show every extreme that they name: `expert_ids`: each row names 8 different experts. Among the rows of one device no expert is named more than 3 times, and in some devices one expert is named exactly 3 times.
All inputs are finite; a program needn't handle non-finite values.
Results may differ from a plain program's by a relative error of at most 0.008.
Values may be sent and summed in bfloat16 or wider, within the bound.
A program may use at most 192 MiB of HBM per device.

v0:
```python
import functools

import jax
import jax.numpy as jnp
from jax import lax
from jax.experimental import pallas as pl
from jax.experimental.pallas import tpu as pltpu
from jax.sharding import PartitionSpec as P

EXPERTS = 16
LANES = 128
F32 = jnp.float32
BF16 = jnp.bfloat16
MESH = pl.DeviceIdType.MESH


def pick(total, sizes):
    for size in sizes:
        if total % size == 0:
            return size
    return total


def factor(chips):
    inner = 1
    while inner * inner * 4 <= chips and chips % (inner * 2) == 0:
        inner *= 2
    return chips // inner, inner


def normed(values, gain_row):
    mean = jnp.mean(values * values, axis=-1, keepdims=True)
    return values * lax.rsqrt(mean + 1e-06) * gain_row


def drain(ref, sem):
    pltpu.make_async_copy(ref, ref, sem).wait()


def kernel(
    n, kq, kc, cb, cw,
    a_hbm, ag_hbm, b_hbm, bg_hbm, ids_hbm, rw_hbm,
    dg_hbm, du_hbm, dd_hbm, eg_hbm, eu_hbm, ed_hbm,
    a_out, b_out,
    a_in, ag_in, b_in, bg_in, ids_in, rw_in,
    gu, dn, gat_b, gat_a, g_acc, u_acc, hid_b, hid_a,
    back_b, back_a,
    in_sem, gu_sem, dn_sem,
    gz_send, gz_recv, gy_send, gy_recv, gc_send, gc_recv,
    s1_send, s1_recv, s2_send, s2_recv, s3_send, s3_recv,
):
    me = lax.axis_index("exp")
    core = lax.rem(me, 2)
    chip = me // 2
    chips = n // 2
    outer, inner = factor(chips)
    p = chip // inner
    q = lax.rem(chip, inner)
    expert = me // (n // EXPERTS)
    rows_a, width = a_in.shape
    rows_b = b_in.shape[0]
    steps = width // kq
    slots = width // cb
    chunks = width // cw
    es = eg_hbm.shape[2]
    fd = dg_hbm.shape[1]
    front = width // 2
    wide = gat_b.shape[3]
    sibling = {"exp": chip * 2 + (1 - core)}

    def line(d):
        return {"exp": (lax.rem(p + d + outer, outer) * inner + q) * 2 + core}

    def cross(e):
        return {"exp": (p * inner + lax.rem(q + e + inner, inner)) * 2 + core}

    def cols(j, size):
        return pl.ds(pl.multiple_of(j * size, size), size)

    def loop(low, high, body):
        def go(i, carry):
            body(i)
            return carry

        lax.fori_loop(low, high, go, 0)

    def signal(target):
        pl.semaphore_signal(barrier, inc=1, device_id=target, device_id_type=MESH)

    barrier = pltpu.get_barrier_semaphore()
    loop(1, outer, lambda d: signal(line(d)))
    loop(1, inner, lambda e: signal(cross(e)))
    signal(sibling)

    inputs = [
        pltpu.make_async_copy(src, dst, in_sem.at[i])
        for i, (src, dst) in enumerate((
            (b_hbm, b_in), (bg_hbm, bg_in), (ids_hbm, ids_in),
            (rw_hbm, rw_in), (a_hbm, a_in), (ag_hbm, ag_in),
        ))
    ]
    for copy in inputs:
        copy.start()

    def gu_slot(ph, w, i):
        return gu.at[w, i, :, pl.ds(0, (es, fd)[ph])]

    def gu_copy(ph, w, i):
        if ph == 0:
            src = (eg_hbm, eu_hbm)[w].at[0, cols(i, kq), :]
        else:
            src = (dg_hbm, du_hbm)[w].at[cols(i, kq), :]
        return pltpu.make_async_copy(src, gu_slot(ph, w, i), gu_sem.at[w, i])

    def dn_place(ph, j):
        return j if ph == 0 else (j + slots) % (slots + slots // 2)

    def dn_slot(ph, j):
        return dn.at[dn_place(ph, j), pl.ds(0, (es, fd)[ph])]

    def dn_copy(ph, j):
        src = ed_hbm.at[0, :, cols(j, cb)] if ph == 0 else dd_hbm.at[:, cols(j, cb)]
        return pltpu.make_async_copy(src, dn_slot(ph, j), dn_sem.at[dn_place(ph, j)])

    def start_gu(ph, i):
        gu_copy(ph, 0, i).start()
        gu_copy(ph, 1, i).start()

    loop(0, steps, lambda i: start_gu(0, i))
    loop(0, slots, lambda j: dn_copy(0, j).start())
    loop(0, slots // 2, lambda j: dn_copy(1, j).start())

    for copy in inputs:
        copy.wait()
    gat_b[0, core, :, pl.ds(0, width)] = normed(b_in[...].astype(F32), bg_in[...]).astype(BF16)
    lane = lax.broadcasted_iota(jnp.int32, (rows_b, LANES), 1)
    table = jnp.zeros((rows_b, LANES), F32)
    for k in range(ids_in.shape[1]):
        table = table + jnp.where(ids_in[:, k : k + 1] == lane, rw_in[:, k : k + 1], 0.0)
    high = table.astype(BF16)
    gat_b[0, core, :, pl.ds(width, LANES)] = high
    gat_b[0, core, :, pl.ds(width + LANES, LANES)] = (table - high.astype(F32)).astype(BF16)
    gat_a[0, core] = normed(a_in[...].astype(F32), ag_in[...]).astype(BF16)

    pl.semaphore_wait(barrier, outer + inner - 1)

    def remote(src, dst, send, recv, target):
        return pltpu.make_async_remote_copy(
            src_ref=src, dst_ref=dst, send_sem=send, recv_sem=recv,
            device_id=target, device_id_type=MESH,
        )

    spans = (pl.ds(0, front), pl.ds(front, wide - front))

    def block(t, s):
        if t < 2:
            return gat_b.at[s, core, :, spans[t]]
        return gat_a.at[s, core]

    def z_copy(t, d):
        return remote(
            block(t, 0), block(t, d * inner), gz_send.at[t], gz_recv.at[t, d], line(-d)
        )

    def y_copy(t, d, e):
        s = d * inner
        return remote(
            block(t, s), block(t, s + e), gy_send.at[t], gy_recv.at[t, s + e], cross(-e)
        )

    def c_copy(t, s):
        own = block(t, s)
        return remote(own, own, gc_send.at[t], gc_recv.at[t], sibling)

    flip = p * 2 >= outer

    def turn(i):
        return jnp.where(flip, outer - i, i)

    def start_line(t):
        loop(1, outer, lambda i: z_copy(t, turn(i)).start())

    def start_own(t):
        loop(1, inner, lambda e: y_copy(t, 0, e).start())
        c_copy(t, 0).start()

    def forward_line(t, low=1, high=outer):
        def go(i):
            d = turn(i)
            z_copy(t, d).wait_recv()
            loop(1, inner, lambda e: y_copy(t, d, e).start())
            c_copy(t, d * inner).start()

        loop(low, high, go)

    def forward_cross(t):
        def go(d):
            def arrived(e):
                y_copy(t, d, e).wait_recv()
                c_copy(t, d * inner + e).start()

            loop(1, inner, arrived)

        loop(0, outer, go)

    def gathered(t):
        if t < 2:
            drain(gat_b.at[:, 1 - core, :, spans[t]], gc_recv.at[t])
        else:
            drain(gat_a.at[:, 1 - core], gc_recv.at[t])

    def rows_of(ph, where):
        buf = (gat_b, gat_a)[ph]
        pieces = [buf[s, c, :, where].astype(F32) for c in range(2) for s in range(chips)]
        return jnp.concatenate(pieces, axis=0)

    def hidden(ph, after):
        used = (es, fd)[ph]
        total = n * (rows_b, rows_a)[ph]
        ga = g_acc.at[pl.ds(0, total), pl.ds(0, used)]
        ua = u_acc.at[pl.ds(0, total), pl.ds(0, used)]
        ga[...] = jnp.zeros(ga.shape, F32)
        ua[...] = jnp.zeros(ua.shape, F32)

        def step(i):
            gu_copy(ph, 0, i).wait()
            gu_copy(ph, 1, i).wait()

            def product(c, gate, up):
                x = rows_of(ph, cols(i * (kq // kc) + c, kc)).astype(BF16)
                at = pl.ds(c * kc, kc) if isinstance(c, int) else cols(c, kc)
                one = jnp.dot(x, gu_slot(ph, 0, i)[at, :], preferred_element_type=F32)
                two = jnp.dot(x, gu_slot(ph, 1, i)[at, :], preferred_element_type=F32)
                return (one, two) if gate is None else (gate + one, up + two)

            if total > 64:
                def small(c):
                    ga[...], ua[...] = product(c, ga[...], ua[...])

                loop(0, kq // kc, small)
            else:
                gate = up = None
                for c in range(kq // kc):
                    gate, up = product(c, gate, up)
                ga[...] += gate
                ua[...] += up
            after(i)

        loop(0, steps, step)
        g = ga[...]
        return (g / (1.0 + jnp.exp(-g)) * ua[...]).astype(BF16)

    def tools(ph):
        mine, s1, r1, keep, ys, yr, own, zs, zr = (back_b, back_a)[ph]
        rows = own.shape[0]
        out = (b_out, a_out)[ph]

        def pair_copy(j):
            where = cols(j, cw)
            return remote(
                s1.at[:, where], r1.at[:, where], s1_send.at[ph], s1_recv.at[ph, j], sibling
            )

        def y_send(j, e):
            where = cols(j, cw)
            return remote(
                ys.at[e - 1, :, :, where], yr.at[e - 1, :, :, where],
                s2_send.at[ph], s2_recv.at[ph, j], cross(e),
            )

        def z_send(j, d):
            where = cols(j, cw)
            return remote(
                zs.at[d - 1, :, where], zr.at[d - 1, :, where],
                s3_send.at[ph], s3_recv.at[ph, j], line(d),
            )

        def pair_done(j):
            where = cols(j, cw)
            pair_copy(j).wait_recv()
            both = mine[:, where] + r1[:, where].astype(F32)
            for d in range(outer):
                at = d * inner * rows
                keep[d, :, where] = both[at : at + rows]
                for e in range(1, inner):
                    ys[e - 1, d, :, where] = both[at + e * rows : at + (e + 1) * rows].astype(BF16)
            loop(1, inner, lambda e: y_send(j, e).start())

        def cross_done(j):
            where = cols(j, cw)
            drain(yr.at[:, :, :, where], s2_recv.at[ph, j])
            for d in range(outer):
                total = keep[d, :, where]
                for e in range(1, inner):
                    total = total + yr[e - 1, d, :, where].astype(F32)
                if d:
                    zs[d - 1, :, where] = total.astype(BF16)
                else:
                    own[:, where] = total
            loop(1, outer, lambda d: z_send(j, d).start())

        def line_done(j):
            where = cols(j, cw)
            drain(zr.at[:, :, where], s3_recv.at[ph, j])
            total = own[:, where]
            for d in range(1, outer):
                total = total + zr[d - 1, :, where].astype(F32)
            out[:, where] = total

        def down(low, high):
            hid = (hid_b, hid_a)[ph]
            loop(low, high, lambda j: dn_copy(ph, j).wait())

            def one(j):
                value = jnp.dot(hid[...], dn_slot(ph, j)[...], preferred_element_type=F32)
                if ph == 0:
                    value = value * scale
                count = mine.shape[0]
                first, second = value[:count], value[count:]
                at = cols(j, cb)
                mine[:, at] = jnp.where(core == 0, first, second)
                s1[:, at] = jnp.where(core == 0, second, first).astype(BF16)

            if n > 32:
                loop(low, high, one)
            else:
                for j in range(low, high):
                    one(j)
            loop(low * cb // cw, high * cb // cw, lambda j: pair_copy(j).start())

        return down, pair_done, cross_done, line_done

    down_b, pair_done_b, cross_done_b, line_done_b = tools(0)
    down_a, pair_done_a, cross_done_a, line_done_a = tools(1)
    mid = chunks // 2

    start_line(0)
    start_own(0)
    forward_line(0, 1, 2)
    start_line(1)
    forward_line(0, 2, outer)
    start_own(1)
    start_line(2)
    forward_cross(0)
    forward_line(1)
    gathered(0)

    def after_b(i):
        start_gu(1, i)

        @pl.when(i == 0)
        def _():
            forward_cross(1)
            start_own(2)
            forward_line(2)

        @pl.when(i == steps // 2 - 1)
        def _():
            gathered(1)

        @pl.when(i == steps // 2)
        def _():
            forward_cross(2)

    hid_b[...] = hidden(0, after_b)
    tables = rows_of(0, pl.ds(width, LANES)) + rows_of(0, pl.ds(width + LANES, LANES))
    chosen = lax.broadcasted_iota(jnp.int32, tables.shape, 1) == expert
    scale = jnp.sum(jnp.where(chosen, tables, 0.0), axis=1, keepdims=True)
    down_b(0, slots // 2)
    loop(slots // 2, slots, lambda j: dn_copy(1, j).start())
    gathered(2)

    def after_a(i):
        @pl.when(i == 0)
        def _():
            loop(0, chunks, pair_done_b)

        @pl.when(i == steps - 1)
        def _():
            loop(0, mid, cross_done_b)

    down_b(slots // 2, slots)
    hid_a[...] = hidden(1, after_a)
    down_a(0, mid)
    loop(mid, chunks - 1, cross_done_b)
    down_a(mid, chunks - 1)
    loop(0, mid, pair_done_a)
    loop(chunks - 1, chunks, cross_done_b)
    down_a(chunks - 1, chunks)
    loop(mid, chunks - 1, pair_done_a)
    loop(0, mid, line_done_b)
    loop(chunks - 1, chunks, pair_done_a)
    loop(0, mid, cross_done_a)
    loop(mid, chunks, line_done_b)
    loop(mid, chunks, cross_done_a)
    loop(0, chunks, line_done_a)

    for t in range(3):
        def sent(count):
            if t < 2:
                return gat_b.at[pl.ds(0, count), 0, :, spans[t]]
            return gat_a.at[pl.ds(0, count), 0]

        drain(sent(outer - 1), gz_send.at[t])
        drain(sent(outer * (inner - 1)), gy_send.at[t])
        drain(sent(chips), gc_send.at[t])
    for ph in range(2):
        s1, ys, zs = (back_b, back_a)[ph][1], (back_b, back_a)[ph][4], (back_b, back_a)[ph][7]
        drain(s1, s1_send.at[ph])
        drain(ys, s2_send.at[ph])
        drain(zs, s3_send.at[ph])


def finish(sum_a, sum_b, a_ref, b_ref, a_out, b_out):
    a_out[...] = (a_ref[...].astype(F32) + sum_a[...]).astype(BF16)
    b_out[...] = (b_ref[...].astype(F32) + sum_b[...]).astype(BF16)


def shards(
    a_tokens, a_gain, dense_gate, dense_up, dense_down, b_tokens, b_gain, expert_ids,
    route_weights, expert_gate, expert_up, expert_down,
):
    n = lax.axis_size("exp")
    chips = n // 2
    outer, inner = factor(chips)
    ra, width = a_tokens.shape
    rb = b_tokens.shape[0]
    fd = dense_gate.shape[1]
    es = expert_gate.shape[2]
    kq = width // 4
    kc = pick(kq, (256, 128))
    cb = cw = width // 4
    steps, slots = width // kq, width // cb
    extra_width = width + 2 * LANES
    most = n * max(ra, rb)

    def back(rows, span):
        return [
            pltpu.VMEM((chips * rows, span), F32),
            pltpu.VMEM((chips * rows, span), BF16),
            pltpu.VMEM((chips * rows, span), BF16),
            pltpu.VMEM((outer, rows, span), F32),
            pltpu.VMEM((inner - 1, outer, rows, span), BF16),
            pltpu.VMEM((inner - 1, outer, rows, span), BF16),
            pltpu.VMEM((rows, span), F32),
            pltpu.VMEM((outer - 1, rows, span), BF16),
            pltpu.VMEM((outer - 1, rows, span), BF16),
        ]

    vmem = pl.BlockSpec(memory_space=pltpu.VMEM)
    hbm = pl.BlockSpec(memory_space=pl.ANY)
    dma = pltpu.SemaphoreType.DMA
    weights = 3 * width * (fd + es)
    gains = (a_gain.reshape(1, width), b_gain.reshape(1, width))
    sums = pl.pallas_call(
        functools.partial(kernel, n, kq, kc, cb, cw),
        out_shape=(
            jax.ShapeDtypeStruct(a_tokens.shape, F32),
            jax.ShapeDtypeStruct(b_tokens.shape, F32),
        ),
        in_specs=[hbm] * 12,
        out_specs=(vmem, vmem),
        scratch_shapes=[
            pltpu.VMEM(a_tokens.shape, BF16),
            pltpu.VMEM((1, width), F32),
            pltpu.VMEM(b_tokens.shape, BF16),
            pltpu.VMEM((1, width), F32),
            pltpu.VMEM(expert_ids.shape, jnp.int32),
            pltpu.VMEM(route_weights.shape, F32),
            pltpu.VMEM((2, steps, kq, max(fd, es)), BF16),
            pltpu.VMEM((slots + slots // 2, max(fd, es), cb), BF16),
            pltpu.VMEM((chips, 2, rb, extra_width), BF16),
            pltpu.VMEM((chips, 2, ra, width), BF16),
            pltpu.VMEM((most, max(fd, es)), F32),
            pltpu.VMEM((most, max(fd, es)), F32),
            pltpu.VMEM((n * rb, es), BF16),
            pltpu.VMEM((n * ra, fd), BF16),
            back(rb, width),
            back(ra, width),
            dma((6,)),
            dma((2, steps)),
            dma((slots + slots // 2,)),
            dma((3,)),
            dma((3, outer)),
            dma((3,)),
            dma((3, chips)),
            dma((3,)),
            dma((3,)),
            dma((2,)),
            dma((2, width // cw)),
            dma((2,)),
            dma((2, width // cw)),
            dma((2,)),
            dma((2, width // cw)),
        ],
        compiler_params=pltpu.CompilerParams(
            collective_id=0, has_side_effects=True, vmem_limit_bytes=67043328
        ),
        cost_estimate=pl.CostEstimate(
            flops=2 * n * max(ra, rb) * weights, bytes_accessed=2 * weights, transcendentals=0
        ),
    )(
        a_tokens, gains[0], b_tokens, gains[1], expert_ids, route_weights,
        dense_gate, dense_up, dense_down, expert_gate, expert_up, expert_down,
    )
    return pl.pallas_call(
        finish,
        out_shape=(
            jax.ShapeDtypeStruct(a_tokens.shape, BF16),
            jax.ShapeDtypeStruct(b_tokens.shape, BF16),
        ),
        in_specs=[vmem] * 4,
        out_specs=(vmem, vmem),
    )(*sums, a_tokens, b_tokens)


def solution(mesh):
    return jax.shard_map(
        shards,
        mesh=mesh,
        in_specs=(
            P(("rep", "exp"), None),
            P(),
            P(None, "exp"),
            P(None, "exp"),
            P("exp", None),
            P(("rep", "exp"), None),
            P(),
            P(("rep", "exp"), None),
            P(("rep", "exp"), None),
            P("exp", None, None),
            P("exp", None, None),
            P("exp", None, None),
        ),
        out_specs=(P(("rep", "exp"), None), P(("rep", "exp"), None)),
        check_vma=False,
    )
```

profile of v0, /device:TPU:0, one launch (start us, length us, event | category | flops | bytes accessed | tf_op | source)
XLA Modules:
  0.0 47.7 jit_solution(8368205576057496350)
XLA Ops:
  0.6 45.5 %shard_map.131 = (f32[2,7168]{1,0:T(2,128)}, f32[4,7168]{1,0:T(4,128)}) custom-call(bf16[2,7168]{1,0:T(2,128)(2,1)} %a_ref.1, f32[1,7168]{1,0:T(1,128)} %bitcast.2, bf16[4,7168]{1,0:T(4,128)(2,1)} %b_ref.1, f32[1,7168]{1,0:T(1,128)} %bitcast.3, s32[4,8]{1,0:T(4,128)} %ids_hbm.1, f32[4,8]{1,0:T(4,128)} %rw_hbm.1, bf16[7168,1152]{1,0:T(8,128)(2,1)} %dg_hbm.1, ...), custom_call_target="tpu_custom_call" | custom-call | flops 5989466112 | bytes 93585408 | tf_op jit(solution)/shard_map/pallas_call | solution.py:455
  46.1 1.6 %shard_map.132 = (bf16[2,7168]{1,0:T(2,128)(2,1)}, bf16[4,7168]{1,0:T(4,128)(2,1)}) custom-call(f32[2,7168]{1,0:T(2,128)} %get-tuple-element.4.sum_a, f32[4,7168]{1,0:T(4,128)} %get-tuple-element.5.sum_b, bf16[2,7168]{1,0:T(2,128)(2,1)} %a_ref.1, bf16[4,7168]{1,0:T(4,128)(2,1)} %b_ref.1), custom_call_target="tpu_custom_call" | custom-call | tf_op jit(solution)/shard_map/pallas_call | solution.py:506
where the time goes:
time: 47.9 us; the launch traced here: 47.7 us
  Pallas kernels  47.1 us (98%)
  between operations  0.64 us (1%)
    pallas_call x1, Pallas kernels, shards(): pl.pallas_call(functools.partial(kernel, n, kq, kc, cb, cw), out_shape=(j...  45.5 us
    pallas_call x1, Pallas kernels, shards(): pl.pallas_call(finish, out_shape=(jax.ShapeDtypeStruct(a_tokens.shape, BF...  1.6 us

commit v1 on v0

--- a/solution.py
+++ b/solution.py
@@ -222,38 +222,44 @@
         ga[...] = jnp.zeros(ga.shape, F32)
         ua[...] = jnp.zeros(ua.shape, F32)
 
+        span = (2, 1)[ph]
+
         def step(i):
-            gu_copy(ph, 0, i).wait()
-            gu_copy(ph, 1, i).wait()
-
-            def product(c, gate, up):
-                x = rows_of(ph, cols(i * (kq // kc) + c, kc)).astype(BF16)
-                at = pl.ds(c * kc, kc) if isinstance(c, int) else cols(c, kc)
-                one = jnp.dot(x, gu_slot(ph, 0, i)[at, :], preferred_element_type=F32)
-                two = jnp.dot(x, gu_slot(ph, 1, i)[at, :], preferred_element_type=F32)
+            for k in range(span):
+                gu_copy(ph, 0, i * span + k).wait()
+                gu_copy(ph, 1, i * span + k).wait()
+
+            def product(k, c, gate, up):
+                at = i * span + k
+                x = rows_of(ph, cols(at * (kq // kc) + c, kc)).astype(BF16)
+                rows = pl.ds(c * kc, kc) if isinstance(c, int) else cols(c, kc)
+                one = jnp.dot(x, gu_slot(ph, 0, at)[rows, :], preferred_element_type=F32)
+                two = jnp.dot(x, gu_slot(ph, 1, at)[rows, :], preferred_element_type=F32)
                 return (one, two) if gate is None else (gate + one, up + two)
 
             if total > 64:
-                def small(c):
-                    ga[...], ua[...] = product(c, ga[...], ua[...])
-
-                loop(0, kq // kc, small)
+                for k in range(span):
+                    def small(c, k=k):
+                        ga[...], ua[...] = product(k, c, ga[...], ua[...])
+
+                    loop(0, kq // kc, small)
             else:
                 gate = up = None
-                for c in range(kq // kc):
-                    gate, up = product(c, gate, up)
+                for k in range(span):
+                    for c in range(kq // kc):
+                        gate, up = product(k, c, gate, up)
                 ga[...] += gate
                 ua[...] += up
             after(i)
 
-        loop(0, steps, step)
+        loop(0, steps // span, step)
         g = ga[...]
         return (g / (1.0 + jnp.exp(-g)) * ua[...]).astype(BF16)
 
     def tools(ph):
         mine, s1, r1, keep, ys, yr, own, zs, zr = (back_b, back_a)[ph]
         rows = own.shape[0]
-        out = (b_out, a_out)[ph]
+        out, tokens = ((b_out, b_in), (a_out, a_in))[ph]
 
         def pair_copy(j):
             where = cols(j, cw)
@@ -305,7 +311,7 @@
             total = own[:, where]
             for d in range(1, outer):
                 total = total + zr[d - 1, :, where].astype(F32)
-            out[:, where] = total
+            out[:, where] = tokens[:, where].astype(F32) + total
 
         def down(low, high):
             hid = (hid_b, hid_a)[ph]
@@ -346,19 +352,17 @@
     gathered(0)
 
     def after_b(i):
-        start_gu(1, i)
+        start_gu(1, 2 * i)
+        start_gu(1, 2 * i + 1)
 
         @pl.when(i == 0)
         def _():
             forward_cross(1)
             start_own(2)
             forward_line(2)
-
-        @pl.when(i == steps // 2 - 1)
-        def _():
             gathered(1)
 
-        @pl.when(i == steps // 2)
+        @pl.when(i == 1)
         def _():
             forward_cross(2)
 
@@ -373,13 +377,14 @@
     def after_a(i):
         @pl.when(i == 0)
         def _():
-            loop(0, chunks, pair_done_b)
-
-        @pl.when(i == steps - 1)
+            loop(mid, chunks, pair_done_b)
+
+        @pl.when(i == steps - 2)
         def _():
             loop(0, mid, cross_done_b)
 
     down_b(slots // 2, slots)
+    loop(0, mid, pair_done_b)
     hid_a[...] = hidden(1, after_a)
     down_a(0, mid)
     loop(mid, chunks - 1, cross_done_b)
@@ -411,9 +416,9 @@
         drain(zs, s3_send.at[ph])
 
 
-def finish(sum_a, sum_b, a_ref, b_ref, a_out, b_out):
-    a_out[...] = (a_ref[...].astype(F32) + sum_a[...]).astype(BF16)
-    b_out[...] = (b_ref[...].astype(F32) + sum_b[...]).astype(BF16)
+def finish(sum_a, sum_b, a_out, b_out):
+    a_out[...] = sum_a[...].astype(BF16)
+    b_out[...] = sum_b[...].astype(BF16)
 
 
 def shards(
@@ -455,8 +460,8 @@
     sums = pl.pallas_call(
         functools.partial(kernel, n, kq, kc, cb, cw),
         out_shape=(
-            jax.ShapeDtypeStruct(a_tokens.shape, F32),
-            jax.ShapeDtypeStruct(b_tokens.shape, F32),
+            pltpu.VMEM(a_tokens.shape, F32),
+            pltpu.VMEM(b_tokens.shape, F32),
         ),
         in_specs=[hbm] * 12,
         out_specs=(vmem, vmem),
@@ -494,7 +499,7 @@
             dma((2, width // cw)),
         ],
         compiler_params=pltpu.CompilerParams(
-            collective_id=0, has_side_effects=True, vmem_limit_bytes=67043328
+            collective_id=0, has_side_effects=True, vmem_limit_bytes=66400000
         ),
         cost_estimate=pl.CostEstimate(
             flops=2 * n * max(ra, rb) * weights, bytes_accessed=2 * weights, transcendentals=0
@@ -509,9 +514,9 @@
             jax.ShapeDtypeStruct(a_tokens.shape, BF16),
             jax.ShapeDtypeStruct(b_tokens.shape, BF16),
         ),
-        in_specs=[vmem] * 4,
+        in_specs=[vmem] * 2,
         out_specs=(vmem, vmem),
-    )(*sums, a_tokens, b_tokens)
+    )(*[pltpu.with_memory_space_constraint(x, pltpu.VMEM) for x in sums])
 
 
 def solution(mesh):

time: 47.9 us -> 44.4 us (0.927)
  Pallas kernels: 47.1 us -> 43.6 us
    pallas_call x1, Pallas kernels: 45.5 us -> 43 us  [shards(): pl.pallas_call(functools.partial(kernel, n, kq, kc, cb, cw), out_shape=(p...]
    pallas_call x1, Pallas kernels: 1.6 us -> 0.66 us  [shards(): pl.pallas_call(finish, out_shape=(jax.ShapeDtypeStruct(a_tokens.shape, BF...]
where the time goes in v1:
time: 44.4 us; the launch traced here: 44.3 us
  Pallas kernels  43.6 us (98%)
  between operations  0.64 us (1%)
    pallas_call x1, Pallas kernels, shards(): pl.pallas_call(functools.partial(kernel, n, kq, kc, cb, cw), out_shape=(p...  43 us

profile of v1, /device:TPU:0, one launch (start us, length us, event | category | flops | bytes accessed | tf_op | source)
XLA Modules:
  0.0 44.3 jit_solution(610622028304195492)
XLA Ops:
  0.6 43.0 %shard_map.131 = (f32[2,7168]{1,0:T(2,128)S(1)}, f32[4,7168]{1,0:T(4,128)S(1)}) custom-call(bf16[2,7168]{1,0:T(2,128)(2,1)} %a_hbm.1, f32[1,7168]{1,0:T(1,128)} %bitcast.2, bf16[4,7168]{1,0:T(4,128)(2,1)} %b_hbm.1, f32[1,7168]{1,0:T(1,128)} %bitcast.3, s32[4,8]{1,0:T(4,128)} %ids_hbm.1, f32[4,8]{1,0:T(4,128)} %rw_hbm.1, bf16[7168,1152]{1,0:T(8,128)(2,1)} %dg_hbm.1, ...), custom_call_target="tpu_custom_call" | custom-call | flops 5989466112 | bytes 93585408 | tf_op jit(solution)/shard_map/pallas_call | solution.py:460
  43.6 0.7 %shard_map.132 = (bf16[2,7168]{1,0:T(2,128)(2,1)}, bf16[4,7168]{1,0:T(4,128)(2,1)}) custom-call(f32[2,7168]{1,0:T(2,128)S(1)} %get-tuple-element.4.sum_a, f32[4,7168]{1,0:T(4,128)S(1)} %get-tuple-element.5.sum_b), custom_call_target="tpu_custom_call" | custom-call | tf_op jit(solution)/shard_map/pallas_call | solution.py:511

commit v2 on v1

--- a/solution.py
+++ b/solution.py
@@ -12,6 +12,7 @@
 F32 = jnp.float32
 BF16 = jnp.bfloat16
 MESH = pl.DeviceIdType.MESH
+FAR = 3
 
 
 def pick(total, sizes):
@@ -44,10 +45,10 @@
     a_out, b_out,
     a_in, ag_in, b_in, bg_in, ids_in, rw_in,
     gu, dn, gat_b, gat_a, g_acc, u_acc, hid_b, hid_a,
-    back_b, back_a,
+    back_b, back_a, far_out, far_in,
     in_sem, gu_sem, dn_sem,
     gz_send, gz_recv, gy_send, gy_recv, gc_send, gc_recv,
-    s1_send, s1_recv, s2_send, s2_recv, s3_send, s3_recv,
+    s1_send, s1_recv, s2_send, s2_recv, s3_send, s3_recv, far_send, far_recv,
 ):
     me = lax.axis_index("exp")
     core = lax.rem(me, 2)
@@ -130,7 +131,7 @@
     loop(0, slots, lambda j: dn_copy(0, j).start())
     loop(0, slots // 2, lambda j: dn_copy(1, j).start())
 
-    for copy in inputs:
+    for copy in inputs[:4]:
         copy.wait()
     gat_b[0, core, :, pl.ds(0, width)] = normed(b_in[...].astype(F32), bg_in[...]).astype(BF16)
     lane = lax.broadcasted_iota(jnp.int32, (rows_b, LANES), 1)
@@ -140,8 +141,6 @@
     high = table.astype(BF16)
     gat_b[0, core, :, pl.ds(width, LANES)] = high
     gat_b[0, core, :, pl.ds(width + LANES, LANES)] = (table - high.astype(F32)).astype(BF16)
-    gat_a[0, core] = normed(a_in[...].astype(F32), ag_in[...]).astype(BF16)
-
     pl.semaphore_wait(barrier, outer + inner - 1)
 
     def remote(src, dst, send, recv, target):
@@ -336,15 +335,59 @@
 
         return down, pair_done, cross_done, line_done
 
+    far = FAR if chips <= 8 else 0
+    near_chunks = chunks - far
+
+    def far_copy(j, s):
+        row = lax.rem(p + s // inner, outer)
+        place = row * inner + lax.rem(q + s % inner, inner)
+        return remote(
+            far_out.at[j - near_chunks, s - 1], far_in.at[j - near_chunks, s - 1],
+            far_send, far_recv.at[j - near_chunks],
+            {"exp": place * 2 + core},
+        )
+
+    def far_start(j):
+        mine, s1, r1 = back_a[:3]
+        where = cols(j, cw)
+        remote(
+            s1.at[:, where], r1.at[:, where], s1_send.at[1], s1_recv.at[1, j], sibling
+        ).wait_recv()
+        both = mine[:, where] + r1[:, where].astype(F32)
+        for s in range(1, chips):
+            far_out[j - near_chunks, s - 1] = both[s * rows_a : (s + 1) * rows_a].astype(BF16)
+        back_a[6][:, where] = both[:rows_a]
+        loop(1, chips, lambda s: far_copy(j, s).start())
+
+    def far_done(j):
+        where = cols(j, cw)
+        drain(far_in.at[j - near_chunks], far_recv.at[j - near_chunks])
+        total = back_a[6][:, where]
+        for s in range(1, chips):
+            total = total + far_in[j - near_chunks, s - 1].astype(F32)
+        a_out[:, where] = a_in[:, where].astype(F32) + total
+
     down_b, pair_done_b, cross_done_b, line_done_b = tools(0)
     down_a, pair_done_a, cross_done_a, line_done_a = tools(1)
     mid = chunks // 2
 
     start_line(0)
     start_own(0)
+    for copy in inputs[4:]:
+        copy.wait()
+    gat_a[0, core] = normed(a_in[...].astype(F32), ag_in[...]).astype(BF16)
     forward_line(0, 1, 2)
-    start_line(1)
+
+    @pl.when(core == 0)
+    def _():
+        start_line(1)
+
     forward_line(0, 2, outer)
+
+    @pl.when(core == 1)
+    def _():
+        start_line(1)
+
     start_own(1)
     start_line(2)
     forward_cross(0)
@@ -386,19 +429,22 @@
     down_b(slots // 2, slots)
     loop(0, mid, pair_done_b)
     hid_a[...] = hidden(1, after_a)
-    down_a(0, mid)
     loop(mid, chunks - 1, cross_done_b)
-    down_a(mid, chunks - 1)
-    loop(0, mid, pair_done_a)
-    loop(chunks - 1, chunks, cross_done_b)
-    down_a(chunks - 1, chunks)
-    loop(mid, chunks - 1, pair_done_a)
+    def pair_sum_a(j):
+        (pair_done_a if j < near_chunks else far_start)(j)
+
+    for j in range(chunks):
+        down_a(j, j + 1)
+        if j == 0:
+            loop(chunks - 1, chunks, cross_done_b)
+        else:
+            pair_sum_a(j - 1)
     loop(0, mid, line_done_b)
-    loop(chunks - 1, chunks, pair_done_a)
-    loop(0, mid, cross_done_a)
+    pair_sum_a(chunks - 1)
     loop(mid, chunks, line_done_b)
-    loop(mid, chunks, cross_done_a)
-    loop(0, chunks, line_done_a)
+    loop(0, near_chunks, cross_done_a)
+    loop(0, near_chunks, line_done_a)
+    loop(near_chunks, chunks, far_done)
 
     for t in range(3):
         def sent(count):
@@ -412,8 +458,12 @@
     for ph in range(2):
         s1, ys, zs = (back_b, back_a)[ph][1], (back_b, back_a)[ph][4], (back_b, back_a)[ph][7]
         drain(s1, s1_send.at[ph])
-        drain(ys, s2_send.at[ph])
-        drain(zs, s3_send.at[ph])
+        near = pl.ds(0, (chunks, near_chunks)[ph] * cw)
+        if (chunks, near_chunks)[ph]:
+            drain(ys.at[:, :, :, near], s2_send.at[ph])
+            drain(zs.at[:, :, near], s3_send.at[ph])
+    if far:
+        drain(far_out, far_send)
 
 
 def finish(sum_a, sum_b, a_out, b_out):
@@ -482,6 +532,8 @@
             pltpu.VMEM((n * ra, fd), BF16),
             back(rb, width),
             back(ra, width),
+            pltpu.VMEM((FAR, chips - 1 if chips <= 8 else 1, ra, cw), BF16),
+            pltpu.VMEM((FAR, chips - 1 if chips <= 8 else 1, ra, cw), BF16),
             dma((6,)),
             dma((2, steps)),
             dma((slots + slots // 2,)),
@@ -497,6 +549,8 @@
             dma((2, width // cw)),
             dma((2,)),
             dma((2, width // cw)),
+            dma,
+            dma((FAR,)),
         ],
         compiler_params=pltpu.CompilerParams(
             collective_id=0, has_side_effects=True, vmem_limit_bytes=66400000

time: 44.4 us -> 42.9 us (0.966)
  Pallas kernels: 43.6 us -> 42.1 us
    pallas_call x1, Pallas kernels: 43 us -> 41.5 us  [shards(): pl.pallas_call(functools.partial(kernel, n, kq, kc, cb, cw), out_shape=(p...]
where the time goes in v2:
time: 42.9 us; the launch traced here: 42.8 us
  Pallas kernels  42.1 us (98%)
  between operations  0.64 us (1%)
    pallas_call x1, Pallas kernels, shards(): pl.pallas_call(functools.partial(kernel, n, kq, kc, cb, cw), out_shape=(p...  41.5 us

profile of v2, /device:TPU:0, one launch (start us, length us, event | category | flops | bytes accessed | tf_op | source)
XLA Modules:
  0.0 42.8 jit_solution(12609215072391172912)
XLA Ops:
  0.6 41.5 %shard_map.131 = (f32[2,7168]{1,0:T(2,128)S(1)}, f32[4,7168]{1,0:T(4,128)S(1)}) custom-call(bf16[2,7168]{1,0:T(2,128)(2,1)} %a_hbm.1, f32[1,7168]{1,0:T(1,128)} %bitcast.2, bf16[4,7168]{1,0:T(4,128)(2,1)} %b_hbm.1, f32[1,7168]{1,0:T(1,128)} %bitcast.3, s32[4,8]{1,0:T(4,128)} %ids_hbm.1, f32[4,8]{1,0:T(4,128)} %rw_hbm.1, bf16[7168,1152]{1,0:T(8,128)(2,1)} %dg_hbm.1, ...), custom_call_target="tpu_custom_call" | custom-call | flops 5989466112 | bytes 93585408 | tf_op jit(solution)/shard_map/pallas_call | solution.py:510
  42.1 0.7 %shard_map.132 = (bf16[2,7168]{1,0:T(2,128)(2,1)}, bf16[4,7168]{1,0:T(4,128)(2,1)}) custom-call(f32[2,7168]{1,0:T(2,128)S(1)} %get-tuple-element.4.sum_a, f32[4,7168]{1,0:T(4,128)S(1)} %get-tuple-element.5.sum_b), custom_call_target="tpu_custom_call" | custom-call | tf_op jit(solution)/shard_map/pallas_call | solution.py:565
